TPU v7x, 32 devices: a whole 2x2x4 slice. The times are simulated.
32 devices in a mesh: head: 4 (over z), outer: 2 (over core), inner: 4 (over y, x).
Axes of the slice: x: 2, y: 2, z: 4, core: 2. Of those that a mesh axis runs over, the one named last changes fastest.
Arguments:
- query: bfloat16 [4096, 8192], P(('outer', 'inner', 'head')), may hold values from -100 to 100
- keys: bfloat16 [4096, 1024], P(('outer', 'inner', 'head')), may hold values from -4.5 to 4.5
- values: bfloat16 [4096, 1024], P(('outer', 'inner', 'head')), may hold values from -6 to 6
- lengths: int32 [8], replicated, may hold values from 1 to 1024, 4096 in all
Outputs:
- attended: bfloat16 [4096, 8192], P(('outer', 'inner', 'head'))
Inputs may be any that keep to these rules, and one draw needn't show every extreme that they name: `lengths`: they sum to 4096, and the longest is exactly 1024.
All inputs are finite; a program needn't handle non-finite values.
Results may differ from a plain program's by a relative error of at most 0.0038.
Values may be sent and summed in bfloat16 or wider, within the bound.
A program may use at most 64 MiB of HBM per device.

v0:
```python
import math

import jax
import jax.numpy as jnp
from jax import lax
from jax.sharding import PartitionSpec as P

HEAD_SIZE = 128


def from_behind(value, axis, steps):
    count = lax.axis_size(axis)
    leading, last = (max(0, -steps), min(count, count - steps))
    return lax.ppermute(value, axis, [(source, source + steps) for source in range(leading, last)])


def doc_numbers(lengths, start_pos, count):
    ends = jnp.cumsum(lengths)
    positions = start_pos + lax.iota(jnp.int32, count)
    numbers = jnp.sum((positions[:, None] >= ends[None, :]).astype(jnp.int32), axis=1)
    return (numbers, positions)


def per_device(query, keys, values, lengths):
    query_local, keys_local, values_local = (
        lax.all_to_all(query, "head", split_axis=1, concat_axis=0, tiled=True),
        lax.all_to_all(keys, "head", split_axis=1, concat_axis=0, tiled=True),
        lax.all_to_all(values, "head", split_axis=1, concat_axis=0, tiled=True),
    )
    local_len = query_local.shape[0]
    pair_heads = keys_local.shape[1] // HEAD_SIZE
    group_width = query_local.shape[1] // keys_local.shape[1]
    context_count = lax.axis_size(("outer", "inner"))
    reach_hops = min(2, context_count // 4)
    position_index = lax.axis_index(("outer", "inner"))
    query_docs, query_pos = doc_numbers(lengths, position_index * local_len, local_len)
    query_groups = jnp.transpose(
        query_local.reshape(local_len, pair_heads, group_width, HEAD_SIZE), (2, 0, 1, 3)
    )
    score_scale = 1.0 / math.sqrt(HEAD_SIZE)

    def attend(state, stacked, distance):
        key_heads = stacked[0].reshape(local_len, pair_heads, HEAD_SIZE)
        value_heads = stacked[1].reshape(local_len, pair_heads, HEAD_SIZE)
        key_docs, key_pos = doc_numbers(lengths, (position_index - distance) * local_len, local_len)
        visible = (
            (query_docs[:, None] == key_docs[None, :])
            & (key_pos[None, :] <= query_pos[:, None])
            & (key_pos[None, :] >= 0)
        )

        def one_group(operands):
            query_part, running_max, running_total, running_sum = operands
            scores = (
                jnp.einsum(
                    "qkd,ckd->kqc", query_part, key_heads, preferred_element_type=jnp.float32
                )
                * score_scale
            )
            masked = jnp.where(visible, scores, -1e30)
            new_max = jnp.maximum(running_max, jnp.max(masked, axis=2))
            weights = jnp.where(visible, jnp.exp(masked - new_max[..., None]), 0.0)
            shrink = jnp.exp(running_max - new_max)
            new_total = running_total * shrink + jnp.sum(weights, axis=2)
            update = jnp.einsum(
                "kqc,ckd->qkd",
                weights.astype(jnp.bfloat16),
                value_heads,
                preferred_element_type=jnp.float32,
            )
            new_sum = running_sum * jnp.transpose(shrink, (1, 0))[..., None] + update
            return (new_max, new_total, new_sum)

        return lax.map(one_group, (query_groups, state[0], state[1], state[2]))

    start_state = (
        jnp.full((group_width, pair_heads, local_len), -1e30, jnp.float32),
        jnp.zeros((group_width, pair_heads, local_len), jnp.float32),
        jnp.zeros((group_width, local_len, pair_heads, HEAD_SIZE), jnp.float32),
    )
    own_pair = jnp.stack((keys_local, values_local))
    state = attend(start_state, own_pair, 0)
    carried = own_pair
    for distance in range(1, reach_hops + 1):
        carried = from_behind(carried, ("outer", "inner"), 1)
        state = attend(state, carried, distance)
    running_max, running_total, running_sum = state
    outcome = running_sum / jnp.transpose(running_total, (0, 2, 1))[..., None]
    outcome = jnp.transpose(outcome, (1, 2, 0, 3))
    outcome = outcome.reshape(local_len, pair_heads * group_width * HEAD_SIZE).astype(jnp.bfloat16)
    return lax.all_to_all(outcome, "head", split_axis=0, concat_axis=1, tiled=True)


def solution(mesh):
    placed = (
        P(("outer", "inner", "head"), None),
        P(("outer", "inner", "head"), None),
        P(("outer", "inner", "head"), None),
        P(),
    )
    return jax.shard_map(
        per_device,
        mesh=mesh,
        in_specs=placed,
        out_specs=P(("outer", "inner", "head"), None),
        check_vma=False,
    )
```

profile of v0, /device:TPU:0, one launch (start us, length us, event | category | flops | bytes accessed | tf_op | source)
XLA Modules:
  0.0 246.9 jit_solution(3934203246122695590)
XLA Ops:
  0.0 1.9 copy.56
  1.9 6.3 %all-to-all-start.1 = ((bf16[128,4,256]{0,2,1:T(8,128)(2,1)}), bf16[128,4,256]{0,2,1:T(8,128)(2,1)S(1)}, u32[]{:S(2)}, u32[]{:S(2)}) async-start(bf16[128,4,256]{0,2,1:T(8,128)(2,1)} %bitcast.2), calls=%async_computation.1 | async-start | bytes 524288 | tf_op jit(solution)/shard_map/all_to_all | solution.py:27
  8.3 1.8 copy.58
  10.1 7.1 %all-to-all-done.1 = bf16[128,4,256]{0,2,1:T(8,128)(2,1)S(1)} async-done(((bf16[128,4,256]{0,2,1:T(8,128)(2,1)}), bf16[128,4,256]{0,2,1:T(8,128)(2,1)S(1)}, u32[]{:S(2)}, u32[]{:S(2)}) %all-to-all-start.1) | async-done | bytes 262176 | tf_op jit(solution)/shard_map/all_to_all | solution.py:27
  17.2 3.4 %all-to-all-start.2 = ((bf16[128,4,256]{0,2,1:T(8,128)(2,1)}), bf16[128,4,256]{0,2,1:T(8,128)(2,1)S(1)}, u32[]{:S(2)}, u32[]{:S(2)}) async-start(bf16[128,4,256]{0,2,1:T(8,128)(2,1)} %bitcast.4), calls=%async_computation.2 | async-start | bytes 524288 | tf_op jit(solution)/shard_map/all_to_all | solution.py:28
  22.2 5.4 %all-to-all-done.2 = bf16[128,4,256]{0,2,1:T(8,128)(2,1)S(1)} async-done(((bf16[128,4,256]{0,2,1:T(8,128)(2,1)}), bf16[128,4,256]{0,2,1:T(8,128)(2,1)S(1)}, u32[]{:S(2)}, u32[]{:S(2)}) %all-to-all-start.2) | async-done | bytes 262176 | tf_op jit(solution)/shard_map/all_to_all | solution.py:28
  27.6 3.6 %all-to-all-start = ((bf16[128,4,2048]{2,0,1:T(8,128)(2,1)}), bf16[128,4,2048]{2,0,1:T(8,128)(2,1)S(1)}, u32[]{:S(2)}, u32[]{:S(2)}) async-start(bf16[128,4,2048]{2,0,1:T(8,128)(2,1)} %bitcast.143), calls=%async_computation | async-start | bytes 4194304 | tf_op jit(solution)/shard_map/all_to_all | solution.py:26
  31.6 4.2 %collective-permute-start = (bf16[2,512,256]{2,1,0:T(8,128)(2,1)S(1)}, bf16[2,512,256]{2,1,0:T(8,128)(2,1)}, u32[]{:S(2)}, u32[]{:S(2)}) collective-permute-start(bf16[2,512,256]{2,1,0:T(8,128)(2,1)S(1)} %pad_maximum_fusion), channel_id=1, source_target_pairs={{0,1},{1,2},{2,3},{3,4},{4,5},{5,6},{6,7},{8,9},{9,10},{10,11},{11... | collective-permute-start | bytes 1572872 | tf_op jit(solution)/shard_map/ppermute | solution.py:14
  35.8 7.3 %collective-permute-done = bf16[2,512,256]{2,1,0:T(8,128)(2,1)} collective-permute-done((bf16[2,512,256]{2,1,0:T(8,128)(2,1)S(1)}, bf16[2,512,256]{2,1,0:T(8,128)(2,1)}, u32[]{:S(2)}, u32[]{:S(2)}) %collective-permute-start) | collective-permute-done | bytes 524320 | tf_op jit(solution)/shard_map/ppermute | solution.py:14
  43.2 5.3 %collective-permute-start.1 = (bf16[2,512,256]{2,1,0:T(8,128)(2,1)}, bf16[2,512,256]{2,1,0:T(8,128)(2,1)}, u32[]{:S(2)}, u32[]{:S(2)}) collective-permute-start(bf16[2,512,256]{2,1,0:T(8,128)(2,1)} %collective-permute-done), channel_id=1, source_target_pairs={{0,1},{1,2},{2,3},{3,4},{4,5},{5,6},{6,7},{8,9},{9,10},{10,11},{11... | collective-permute-start | bytes 1572872 | tf_op jit(solution)/shard_map/ppermute | solution.py:14
  52.1 5.0 %collective-permute-done.1 = bf16[2,512,256]{2,1,0:T(8,128)(2,1)} collective-permute-done((bf16[2,512,256]{2,1,0:T(8,128)(2,1)}, bf16[2,512,256]{2,1,0:T(8,128)(2,1)}, u32[]{:S(2)}, u32[]{:S(2)}) %collective-permute-start.1) | collective-permute-done | bytes 524320 | tf_op jit(solution)/shard_map/ppermute | solution.py:14
  58.8 17.9 %all-to-all-done = bf16[128,4,2048]{2,0,1:T(8,128)(2,1)S(1)} async-done(((bf16[128,4,2048]{2,0,1:T(8,128)(2,1)}), bf16[128,4,2048]{2,0,1:T(8,128)(2,1)S(1)}, u32[]{:S(2)}, u32[]{:S(2)}) %all-to-all-start) | async-done | bytes 2097184 | tf_op jit(solution)/shard_map/all_to_all | solution.py:26
  77.8 2.4 broadcast.125.clone.1
  80.3 27.0 %while.43 = (s32[]{:T(128)}, f32[8,2,512]{2,1,0:T(2,128)S(1)}, f32[8,2,512]{2,1,0:T(2,128)S(1)}, f32[8,512,2,128]{3,1,2,0:T(8,128)}, bf16[8,512,2,128]{3,1,2,0:T...) while((s32[]{:T(128)}, f32[8,2,512]{2,1,0:T(2,128)S(1)}, ...), condition=%wide.region_5.6_spmd.clone, body=%wide.region_2.0_spmd.clone.sunk | while | flops 276435968 | bytes 9753745 | solution.py:74
  81.4 1.8 fusion.111
  84.7 1.8 fusion.111
  88.1 1.8 fusion.111
  91.5 1.8 fusion.111
  94.8 1.8 fusion.111
  98.2 1.8 fusion.111
  101.5 1.8 fusion.111
  104.8 1.8 fusion.111
  107.2 2.4 broadcast.125.clone
  109.6 34.8 %while.44 = (s32[]{:T(128)}, f32[8,2,512]{2,1,0:T(2,128)S(1)}, f32[8,2,512]{2,1,0:T(2,128)S(1)}, f32[8,512,2,128]{3,1,2,0:T(8,128)}, f32[8,2,512]{2,1,0:T(2,128)...) while((s32[]{:T(128)}, f32[8,2,512]{2,1,0:T(2,128)S(1)}, ...), condition=%wide.region_10.11_spmd.clone, body=%wide.region_7.10_spmd.clone.sunk | while | flops 276566016 | bytes 9245857 | solution.py:74
  110.6 2.8 %fusion.119 = f32[8,512,2,128]{3,1,2,0:T(8,128)} fusion(f32[8,512,2,128]{3,1,2,0:T(8,128)} %get-tuple-element.807, s32[]{:T(128)} %get-tuple-element.804, bf16[512,2,128]{2,0,1:T(8,128)(2,1)S(1)} %get-tuple-element.829, f32[2,512,512]{1,2,0:T(8,128)S(1)} %get-tuple-element.731, f32[2,512]{1,0:T(2,128)S(1)} %get-tuple-element.733, ...), kind=kOutput, calls=%fused_computation.40.clone.1 | convolution fusion | flops 137101312 | bytes 3678720 | tf_op jit(solution)/shard_map/while/body/eval_jaxpr/kqc,ckd->qkd/dot_general | solution.py:65
  114.9 2.8 %fusion.119 = f32[8,512,2,128]{3,1,2,0:T(8,128)} fusion(f32[8,512,2,128]{3,1,2,0:T(8,128)} %get-tuple-element.807, s32[]{:T(128)} %get-tuple-element.804, bf16[512,2,128]{2,0,1:T(8,128)(2,1)S(1)} %get-tuple-element.829, f32[2,512,512]{1,2,0:T(8,128)S(1)} %get-tuple-element.731, f32[2,512]{1,0:T(2,128)S(1)} %get-tuple-element.733, ...), kind=kOutput, calls=%fused_computation.40.clone.1 | convolution fusion | flops 137101312 | bytes 3678720 | tf_op jit(solution)/shard_map/while/body/eval_jaxpr/kqc,ckd->qkd/dot_general | solution.py:65
  119.2 2.8 %fusion.119 = f32[8,512,2,128]{3,1,2,0:T(8,128)} fusion(f32[8,512,2,128]{3,1,2,0:T(8,128)} %get-tuple-element.807, s32[]{:T(128)} %get-tuple-element.804, bf16[512,2,128]{2,0,1:T(8,128)(2,1)S(1)} %get-tuple-element.829, f32[2,512,512]{1,2,0:T(8,128)S(1)} %get-tuple-element.731, f32[2,512]{1,0:T(2,128)S(1)} %get-tuple-element.733, ...), kind=kOutput, calls=%fused_computation.40.clone.1 | convolution fusion | flops 137101312 | bytes 3678720 | tf_op jit(solution)/shard_map/while/body/eval_jaxpr/kqc,ckd->qkd/dot_general | solution.py:65
  123.6 2.8 %fusion.119 = f32[8,512,2,128]{3,1,2,0:T(8,128)} fusion(f32[8,512,2,128]{3,1,2,0:T(8,128)} %get-tuple-element.807, s32[]{:T(128)} %get-tuple-element.804, bf16[512,2,128]{2,0,1:T(8,128)(2,1)S(1)} %get-tuple-element.829, f32[2,512,512]{1,2,0:T(8,128)S(1)} %get-tuple-element.731, f32[2,512]{1,0:T(2,128)S(1)} %get-tuple-element.733, ...), kind=kOutput, calls=%fused_computation.40.clone.1 | convolution fusion | flops 137101312 | bytes 3678720 | tf_op jit(solution)/shard_map/while/body/eval_jaxpr/kqc,ckd->qkd/dot_general | solution.py:65
  128.0 2.8 %fusion.119 = f32[8,512,2,128]{3,1,2,0:T(8,128)} fusion(f32[8,512,2,128]{3,1,2,0:T(8,128)} %get-tuple-element.807, s32[]{:T(128)} %get-tuple-element.804, bf16[512,2,128]{2,0,1:T(8,128)(2,1)S(1)} %get-tuple-element.829, f32[2,512,512]{1,2,0:T(8,128)S(1)} %get-tuple-element.731, f32[2,512]{1,0:T(2,128)S(1)} %get-tuple-element.733, ...), kind=kOutput, calls=%fused_computation.40.clone.1 | convolution fusion | flops 137101312 | bytes 3678720 | tf_op jit(solution)/shard_map/while/body/eval_jaxpr/kqc,ckd->qkd/dot_general | solution.py:65
  132.3 2.8 %fusion.119 = f32[8,512,2,128]{3,1,2,0:T(8,128)} fusion(f32[8,512,2,128]{3,1,2,0:T(8,128)} %get-tuple-element.807, s32[]{:T(128)} %get-tuple-element.804, bf16[512,2,128]{2,0,1:T(8,128)(2,1)S(1)} %get-tuple-element.829, f32[2,512,512]{1,2,0:T(8,128)S(1)} %get-tuple-element.731, f32[2,512]{1,0:T(2,128)S(1)} %get-tuple-element.733, ...), kind=kOutput, calls=%fused_computation.40.clone.1 | convolution fusion | flops 137101312 | bytes 3678720 | tf_op jit(solution)/shard_map/while/body/eval_jaxpr/kqc,ckd->qkd/dot_general | solution.py:65
  136.6 2.8 %fusion.119 = f32[8,512,2,128]{3,1,2,0:T(8,128)} fusion(f32[8,512,2,128]{3,1,2,0:T(8,128)} %get-tuple-element.807, s32[]{:T(128)} %get-tuple-element.804, bf16[512,2,128]{2,0,1:T(8,128)(2,1)S(1)} %get-tuple-element.829, f32[2,512,512]{1,2,0:T(8,128)S(1)} %get-tuple-element.731, f32[2,512]{1,0:T(2,128)S(1)} %get-tuple-element.733, ...), kind=kOutput, calls=%fused_computation.40.clone.1 | convolution fusion | flops 137101312 | bytes 3678720 | tf_op jit(solution)/shard_map/while/body/eval_jaxpr/kqc,ckd->qkd/dot_general | solution.py:65
  141.0 2.8 %fusion.119 = f32[8,512,2,128]{3,1,2,0:T(8,128)} fusion(f32[8,512,2,128]{3,1,2,0:T(8,128)} %get-tuple-element.807, s32[]{:T(128)} %get-tuple-element.804, bf16[512,2,128]{2,0,1:T(8,128)(2,1)S(1)} %get-tuple-element.829, f32[2,512,512]{1,2,0:T(8,128)S(1)} %get-tuple-element.731, f32[2,512]{1,0:T(2,128)S(1)} %get-tuple-element.733, ...), kind=kOutput, calls=%fused_computation.40.clone.1 | convolution fusion | flops 137101312 | bytes 3678720 | tf_op jit(solution)/shard_map/while/body/eval_jaxpr/kqc,ckd->qkd/dot_general | solution.py:65
  144.4 2.4 broadcast.125
  146.8 34.8 %while.45 = (s32[]{:T(128)}, f32[8,2,512]{2,1,0:T(2,128)S(1)}, f32[8,512,2,128]{3,1,2,0:T(8,128)}, f32[8,2,512]{2,1,0:T(2,128)S(1)}, f32[8,2,512]{2,1,0:T(2,128)...) while((s32[]{:T(128)}, f32[8,2,512]{2,1,0:T(2,128)S(1)}, ...), condition=%wide.region_15.16_spmd.clone, body=%wide.region_12.15_spmd.clone.sunk | while | flops 276566016 | bytes 9241753 | solution.py:74
  147.8 2.8 %fusion.127 = f32[8,512,2,128]{3,1,2,0:T(8,128)} fusion(f32[8,512,2,128]{3,1,2,0:T(8,128)} %get-tuple-element.853, s32[]{:T(128)} %get-tuple-element.851, bf16[512,2,128]{2,0,1:T(8,128)(2,1)S(1)} %get-tuple-element.874, f32[2,512,512]{1,2,0:T(8,128)S(1)} %get-tuple-element.751, f32[2,512]{1,0:T(2,128)S(1)} %get-tuple-element.753, ...), kind=kOutput, calls=%fused_computation.71.clone.1 | convolution fusion | flops 137101312 | bytes 3678720 | tf_op jit(solution)/shard_map/while/body/eval_jaxpr/kqc,ckd->qkd/dot_general | solution.py:65
  152.1 2.8 %fusion.127 = f32[8,512,2,128]{3,1,2,0:T(8,128)} fusion(f32[8,512,2,128]{3,1,2,0:T(8,128)} %get-tuple-element.853, s32[]{:T(128)} %get-tuple-element.851, bf16[512,2,128]{2,0,1:T(8,128)(2,1)S(1)} %get-tuple-element.874, f32[2,512,512]{1,2,0:T(8,128)S(1)} %get-tuple-element.751, f32[2,512]{1,0:T(2,128)S(1)} %get-tuple-element.753, ...), kind=kOutput, calls=%fused_computation.71.clone.1 | convolution fusion | flops 137101312 | bytes 3678720 | tf_op jit(solution)/shard_map/while/body/eval_jaxpr/kqc,ckd->qkd/dot_general | solution.py:65
  156.4 2.8 %fusion.127 = f32[8,512,2,128]{3,1,2,0:T(8,128)} fusion(f32[8,512,2,128]{3,1,2,0:T(8,128)} %get-tuple-element.853, s32[]{:T(128)} %get-tuple-element.851, bf16[512,2,128]{2,0,1:T(8,128)(2,1)S(1)} %get-tuple-element.874, f32[2,512,512]{1,2,0:T(8,128)S(1)} %get-tuple-element.751, f32[2,512]{1,0:T(2,128)S(1)} %get-tuple-element.753, ...), kind=kOutput, calls=%fused_computation.71.clone.1 | convolution fusion | flops 137101312 | bytes 3678720 | tf_op jit(solution)/shard_map/while/body/eval_jaxpr/kqc,ckd->qkd/dot_general | solution.py:65
  160.8 2.8 %fusion.127 = f32[8,512,2,128]{3,1,2,0:T(8,128)} fusion(f32[8,512,2,128]{3,1,2,0:T(8,128)} %get-tuple-element.853, s32[]{:T(128)} %get-tuple-element.851, bf16[512,2,128]{2,0,1:T(8,128)(2,1)S(1)} %get-tuple-element.874, f32[2,512,512]{1,2,0:T(8,128)S(1)} %get-tuple-element.751, f32[2,512]{1,0:T(2,128)S(1)} %get-tuple-element.753, ...), kind=kOutput, calls=%fused_computation.71.clone.1 | convolution fusion | flops 137101312 | bytes 3678720 | tf_op jit(solution)/shard_map/while/body/eval_jaxpr/kqc,ckd->qkd/dot_general | solution.py:65
  165.1 2.8 %fusion.127 = f32[8,512,2,128]{3,1,2,0:T(8,128)} fusion(f32[8,512,2,128]{3,1,2,0:T(8,128)} %get-tuple-element.853, s32[]{:T(128)} %get-tuple-element.851, bf16[512,2,128]{2,0,1:T(8,128)(2,1)S(1)} %get-tuple-element.874, f32[2,512,512]{1,2,0:T(8,128)S(1)} %get-tuple-element.751, f32[2,512]{1,0:T(2,128)S(1)} %get-tuple-element.753, ...), kind=kOutput, calls=%fused_computation.71.clone.1 | convolution fusion | flops 137101312 | bytes 3678720 | tf_op jit(solution)/shard_map/while/body/eval_jaxpr/kqc,ckd->qkd/dot_general | solution.py:65
  169.5 2.9 %fusion.127 = f32[8,512,2,128]{3,1,2,0:T(8,128)} fusion(f32[8,512,2,128]{3,1,2,0:T(8,128)} %get-tuple-element.853, s32[]{:T(128)} %get-tuple-element.851, bf16[512,2,128]{2,0,1:T(8,128)(2,1)S(1)} %get-tuple-element.874, f32[2,512,512]{1,2,0:T(8,128)S(1)} %get-tuple-element.751, f32[2,512]{1,0:T(2,128)S(1)} %get-tuple-element.753, ...), kind=kOutput, calls=%fused_computation.71.clone.1 | convolution fusion | flops 137101312 | bytes 3678720 | tf_op jit(solution)/shard_map/while/body/eval_jaxpr/kqc,ckd->qkd/dot_general | solution.py:65
  173.8 2.8 %fusion.127 = f32[8,512,2,128]{3,1,2,0:T(8,128)} fusion(f32[8,512,2,128]{3,1,2,0:T(8,128)} %get-tuple-element.853, s32[]{:T(128)} %get-tuple-element.851, bf16[512,2,128]{2,0,1:T(8,128)(2,1)S(1)} %get-tuple-element.874, f32[2,512,512]{1,2,0:T(8,128)S(1)} %get-tuple-element.751, f32[2,512]{1,0:T(2,128)S(1)} %get-tuple-element.753, ...), kind=kOutput, calls=%fused_computation.71.clone.1 | convolution fusion | flops 137101312 | bytes 3678720 | tf_op jit(solution)/shard_map/while/body/eval_jaxpr/kqc,ckd->qkd/dot_general | solution.py:65
  178.2 2.8 %fusion.127 = f32[8,512,2,128]{3,1,2,0:T(8,128)} fusion(f32[8,512,2,128]{3,1,2,0:T(8,128)} %get-tuple-element.853, s32[]{:T(128)} %get-tuple-element.851, bf16[512,2,128]{2,0,1:T(8,128)(2,1)S(1)} %get-tuple-element.874, f32[2,512,512]{1,2,0:T(8,128)S(1)} %get-tuple-element.751, f32[2,512]{1,0:T(2,128)S(1)} %get-tuple-element.753, ...), kind=kOutput, calls=%fused_computation.71.clone.1 | convolution fusion | flops 137101312 | bytes 3678720 | tf_op jit(solution)/shard_map/while/body/eval_jaxpr/kqc,ckd->qkd/dot_general | solution.py:65
  181.6 2.9 %fusion.73 = bf16[512,2,8,128]{3,0,1,2:T(8,128)(2,1)S(1)} fusion(f32[8,512,2,128]{3,1,2,0:T(8,128)} %get-tuple-element.167, f32[8,512,2]{1,2,0:T(2,128)S(1)} %bitcast.213), kind=kLoop, calls=%fused_computation.96 | loop fusion | flops 2097152 | bytes 6324224 | tf_op jit(solution)/shard_map/convert_element_type | solution.py:90
  184.5 2.7 %copy.75 = bf16[512,2,8,128]{3,2,1,0:T(8,128)(2,1)} copy(bf16[512,2,8,128]{3,0,1,2:T(8,128)(2,1)S(1)} %fusion.73) | data formatting | bytes 4194304 | tf_op jit(solution)/shard_map/convert_element_type | solution.py:90
  187.1 2.8 %convert_element_type.34 = bf16[4,128,2048]{2,1,0:T(8,128)(2,1)S(1)} reshape(bf16[512,2,8,128]{3,2,1,0:T(8,128)(2,1)} %copy.75) | data formatting | bytes 4194304 | tf_op jit(solution)/shard_map/convert_element_type | solution.py:90
  190.0 51.0 %all_to_all.64 = bf16[4,128,2048]{2,1,0:T(8,128)(2,1)} all-to-all(bf16[4,128,2048]{2,1,0:T(8,128)(2,1)S(1)} %convert_element_type.34), channel_id=1, replica_groups=mesh['head'=4,'outer'=2,'inner'=4] {'head'}, dimensions={0} | all-to-all | bytes 4194304 | tf_op jit(solution)/shard_map/all_to_all | solution.py:91
  241.0 3.0 %copy.76 = bf16[128,4,2048]{0,2,1:T(8,128)(2,1)S(1)} copy(bf16[128,4,2048]{2,0,1:T(8,128)(2,1)} %bitcast.202) | data formatting | bytes 4194304 | tf_op jit(solution)/shard_map/all_to_all | solution.py:91
  244.0 2.9 %copy.77 = bf16[128,8192]{1,0:T(8,128)(2,1)} copy(bf16[128,8192]{0,1:T(8,128)(2,1)S(1)} %bitcast.203) | data formatting | bytes 4194304 | tf_op jit(solution)/shard_map/all_to_all | solution.py:91
  (174 shorter events, 44.0 us)
Async XLA Ops:
  0.0 20.6 %copy-start = (bf16[128,8192]{1,0:T(8,128)(2,1)S(1)}, bf16[128,8192]{1,0:T(8,128)(2,1)}, u32[]{:S(2)}) copy-start(bf16[128,8192]{1,0:T(8,128)(2,1)} %param.10) | copy-start | bytes 6291460
  1.9 15.3 %all-to-all-start.1 = ((bf16[128,4,256]{0,2,1:T(8,128)(2,1)}), bf16[128,4,256]{0,2,1:T(8,128)(2,1)S(1)}, u32[]{:S(2)}, u32[]{:S(2)}) async-start(bf16[128,4,256]{0,2,1:T(8,128)(2,1)} %bitcast.2), calls=%async_computation.1 | async-start | bytes 524288 | tf_op jit(solution)/shard_map/all_to_all | solution.py:27
  17.2 10.4 %all-to-all-start.2 = ((bf16[128,4,256]{0,2,1:T(8,128)(2,1)}), bf16[128,4,256]{0,2,1:T(8,128)(2,1)S(1)}, u32[]{:S(2)}, u32[]{:S(2)}) async-start(bf16[128,4,256]{0,2,1:T(8,128)(2,1)} %bitcast.4), calls=%async_computation.2 | async-start | bytes 524288 | tf_op jit(solution)/shard_map/all_to_all | solution.py:28
  27.6 49.0 %all-to-all-start = ((bf16[128,4,2048]{2,0,1:T(8,128)(2,1)}), bf16[128,4,2048]{2,0,1:T(8,128)(2,1)S(1)}, u32[]{:S(2)}, u32[]{:S(2)}) async-start(bf16[128,4,2048]{2,0,1:T(8,128)(2,1)} %bitcast.143), calls=%async_computation | async-start | bytes 4194304 | tf_op jit(solution)/shard_map/all_to_all | solution.py:26
  31.2 17.2 %copy-start.3 = (s32[8]{0:T(128)S(1)}, s32[8]{0:T(128)}, u32[]{:S(2)}) copy-start(s32[8]{0:T(128)} %param.13) | copy-start | bytes 100
  31.6 11.6 %collective-permute-start = (bf16[2,512,256]{2,1,0:T(8,128)(2,1)S(1)}, bf16[2,512,256]{2,1,0:T(8,128)(2,1)}, u32[]{:S(2)}, u32[]{:S(2)}) collective-permute-start(bf16[2,512,256]{2,1,0:T(8,128)(2,1)S(1)} %pad_maximum_fusion), channel_id=1, source_target_pairs={{0,1},{1,2},{2,3},{3,4},{4,5},{5,6},{6,7},{8,9},{9,10},{10,11},{11... | collective-permute-start | bytes 1572872 | tf_op jit(solution)/shard_map/ppermute | solution.py:14
  43.2 13.9 %collective-permute-start.1 = (bf16[2,512,256]{2,1,0:T(8,128)(2,1)}, bf16[2,512,256]{2,1,0:T(8,128)(2,1)}, u32[]{:S(2)}, u32[]{:S(2)}) collective-permute-start(bf16[2,512,256]{2,1,0:T(8,128)(2,1)} %collective-permute-done), channel_id=1, source_target_pairs={{0,1},{1,2},{2,3},{3,4},{4,5},{5,6},{6,7},{8,9},{9,10},{10,11},{11... | collective-permute-start | bytes 1572872 | tf_op jit(solution)/shard_map/ppermute | solution.py:14
  80.5 1.0 copy-start.2
  83.8 1.0 copy-start.2
  87.2 1.0 copy-start.2
  90.5 1.0 copy-start.2
  93.9 1.0 copy-start.2
  97.2 1.0 copy-start.2
  100.6 1.0 copy-start.2
  103.9 1.0 copy-start.2
  107.2 2.4 copy-start.1
where the time goes:
time: 249 us; the launch traced here: 247 us
  matrix products  73 us (29%)
  blocking collectives  51 us (20%)
  waiting for transfers between devices  42.7 us (17%)
  local copies, waits for them, and re-layouts  30.7 us (12%)
  other arithmetic  25.2 us (10%)
  starting transfers between devices  22.9 us (9%)
    dot_general x24, matrix products, one_group(): jnp.einsum('kqc,ckd->qkd', weights.astype(jnp.bfloat16), value_heads, pre...  59.7 us
    all_to_all x1, blocking collectives, per_device(): lax.all_to_all(outcome, 'head', split_axis=0, concat_axis=1, tiled=True)  51 us
    all_to_all x1, waiting for transfers between devices, per_device(): lax.all_to_all(query, 'head', split_axis=1, concat_axis=0, tiled=True)  17.9 us
    reduce_sum x24, other arithmetic, one_group(): new_total = running_total * shrink + jnp.sum(weights, axis=2)  13.5 us
    dot_general x24, matrix products, one_group(): jnp.einsum('qkd,ckd->kqc', query_part, key_heads, preferred_element_type=...  13.3 us
    ppermute x2, waiting for transfers between devices, from_behind(): lax.ppermute(value, axis, [(source, source + steps) for source in range(l...  12.3 us
    ppermute x2, starting transfers between devices, from_behind(): lax.ppermute(value, axis, [(source, source + steps) for source in range(l...  9.49 us
    and x24, other arithmetic, attend(): (query_docs[:, None] == key_docs[None, :]) & (key_pos[None, :] <= query_p...  7.46 us
  transfers between devices with their start and end apart: 5, of which 5 were waited for; matrix products, arithmetic and copies ran while one was open for 4% of the time, Pallas kernels for 0%

commit v1 on v0

v1 whole, which is shorter than its diff:
```python
import functools
import math

import jax
import jax.numpy as jnp
from jax import lax
from jax.experimental import pallas as pl
from jax.experimental.pallas import tpu as pltpu
from jax.sharding import PartitionSpec as P

HEAD_SIZE = 128
MESH = pl.DeviceIdType.MESH


def kernel(
    heads, outers, inners, lengths_ref, q_ref, k_ref, v_ref, out_ref,
    kv, bias, own_sem, z_send, z_recv, y_send, y_recv, x_send, x_recv,
):
    tokens = q_ref.shape[0]
    groups = k_ref.shape[1] // HEAD_SIZE
    width = q_ref.shape[1] // k_ref.shape[1]
    block = heads * tokens
    contexts = outers * inners
    span = (2 * heads + 1) * tokens
    me = lax.axis_index("head")
    ctx = lax.axis_index("outer") * inners + lax.axis_index("inner")
    odd = lax.rem(ctx, 2)

    def context(steps):
        at = lax.rem(ctx + steps + contexts, contexts)
        return {"outer": at // inners, "inner": lax.rem(at, inners)}

    partner = context(1 - 2 * odd)

    def own_copy(g, which):
        ref = (k_ref, v_ref)[which]
        return pltpu.make_async_copy(
            ref.at[:, pl.ds(pl.multiple_of(g * HEAD_SIZE, HEAD_SIZE), HEAD_SIZE)],
            kv.at[g, which, pl.ds(pl.multiple_of(2 * block + me * tokens, tokens), tokens), :],
            own_sem.at[which, g],
        )

    def z_copy(g, distance):
        rows = pl.ds(pl.multiple_of(2 * block + me * tokens, tokens), tokens)
        return pltpu.make_async_remote_copy(
            src_ref=kv.at[g, :, rows, :],
            dst_ref=kv.at[g, :, rows, :],
            send_sem=z_send.at[distance, g],
            recv_sem=z_recv.at[distance, g],
            device_id={"head": lax.rem(me + distance, heads)},
            device_id_type=MESH,
        )

    def z_arrival(g, distance):
        source = lax.rem(me - distance + heads, heads)
        rows = pl.ds(pl.multiple_of(2 * block + source * tokens, tokens), tokens)
        return pltpu.make_async_remote_copy(
            src_ref=kv.at[g, :, rows, :],
            dst_ref=kv.at[g, :, rows, :],
            send_sem=z_send.at[distance, g],
            recv_sem=z_recv.at[distance, g],
            device_id={"head": lax.rem(me + distance, heads)},
            device_id_type=MESH,
        )

    def y_copy(g):
        return pltpu.make_async_remote_copy(
            src_ref=kv.at[g, :, pl.ds(2 * block, block), :],
            dst_ref=kv.at[g, :, pl.ds(0, block), :],
            send_sem=y_send.at[g],
            recv_sem=y_recv.at[g],
            device_id=context(2),
            device_id_type=MESH,
        )

    def x_copy(g):
        start = pl.multiple_of((1 - odd) * 2 * block, block)
        return pltpu.make_async_remote_copy(
            src_ref=kv.at[g, :, pl.ds(start, block), :],
            dst_ref=kv.at[g, :, pl.ds(block, block), :],
            send_sem=x_send.at[g],
            recv_sem=x_recv.at[g],
            device_id=partner,
            device_id_type=MESH,
        )

    for g in range(groups):
        own_copy(g, 0).start()
        own_copy(g, 1).start()

    barrier = pltpu.get_barrier_semaphore()
    for distance in range(1, heads):
        pl.semaphore_signal(
            barrier, inc=1, device_id={"head": lax.rem(me + distance, heads)}, device_id_type=MESH
        )
    for place in (context(2), context(-2), partner):
        pl.semaphore_signal(barrier, inc=1, device_id=place, device_id_type=MESH)
    pl.semaphore_wait(barrier, heads - 1 + 3)

    for g in range(groups):
        own_copy(g, 0).wait()
        own_copy(g, 1).wait()
        for distance in range(1, heads):
            z_copy(g, distance).start()

    first = ctx * block + me * tokens
    query_pos = first + lax.broadcasted_iota(jnp.int32, (tokens, span), 0)
    key_pos = first - 2 * block + lax.broadcasted_iota(jnp.int32, (tokens, span), 1)
    row_pos = first + lax.broadcasted_iota(jnp.int32, (tokens, 128), 0)
    begin = jnp.zeros((tokens, 128), jnp.int32)
    end = jnp.int32(0)
    for n in range(lengths_ref.shape[0]):
        end = end + lengths_ref[n]
        begin = jnp.where(row_pos >= end, end, begin)
    visible = (key_pos >= begin[:, :1]) & (key_pos <= query_pos)
    bias[...] = jnp.where(visible, 0.0, -1e30)

    factor = math.log2(math.e) / math.sqrt(HEAD_SIZE)
    pair = 2 if width % 2 == 0 else 1
    reading = pl.ds(pl.multiple_of(me * tokens, tokens), span)

    def compute(g):
        key_part = kv.at[g, 0]
        value_part = kv.at[g, 1]

        def heads_of(j, carry):
            at = (g * width + j * pair) * HEAD_SIZE
            columns = [
                pl.ds(pl.multiple_of(at + p * HEAD_SIZE, HEAD_SIZE), HEAD_SIZE) for p in range(pair)
            ]
            q = jnp.concatenate([q_ref[:, c] for c in columns], axis=0)
            scores = lax.dot_general(
                q, key_part[reading, :], (((1,), (1,)), ((), ())), preferred_element_type=jnp.float32
            )
            scores = scores.reshape(pair, tokens, span) + bias[...][None]
            scores = scores.reshape(pair * tokens, span)
            top = jnp.max(scores, axis=1, keepdims=True)
            weights = jnp.exp2((scores - top) * factor)
            total = jnp.sum(weights, axis=1, keepdims=True)
            summed = jnp.dot(
                weights.astype(jnp.bfloat16), value_part[reading, :],
                preferred_element_type=jnp.float32,
            )
            result = (summed / total).astype(out_ref.dtype)
            for p in range(pair):
                out_ref[:, columns[p]] = result[p * tokens:(p + 1) * tokens]
            return carry

        lax.fori_loop(0, width // pair, heads_of, 0)

    def step(t, carry):
        @pl.when(t < groups)
        def _():
            for distance in range(1, heads):
                z_arrival(t, distance).wait_recv()
            y_copy(t).start()

            @pl.when(odd == 0)
            def _():
                x_copy(t).start()

        @pl.when((t >= 1) & (t < groups + 1))
        def _():
            y_copy(t - 1).wait_recv()

            @pl.when(odd == 1)
            def _():
                x_copy(t - 1).start()

        @pl.when(t >= 2)
        def _():
            x_copy(t - 2).wait_recv()
            compute(t - 2)

        return carry

    lax.fori_loop(0, groups + 2, step, 0)

    def drain(g, carry):
        for distance in range(1, heads):
            z_copy(g, distance).wait_send()
        y_copy(g).wait_send()
        x_copy(g).wait_send()
        return carry

    lax.fori_loop(0, groups, drain, 0)


def solution(mesh):
    heads, outers, inners = (mesh.shape[name] for name in ("head", "outer", "inner"))

    def per_device(query, keys, values, lengths):
        tokens = query.shape[0]
        groups = keys.shape[1] // HEAD_SIZE
        return pl.pallas_call(
            functools.partial(kernel, heads, outers, inners),
            out_shape=jax.ShapeDtypeStruct(query.shape, query.dtype),
            in_specs=[
                pl.BlockSpec(memory_space=pltpu.SMEM),
                pl.BlockSpec(memory_space=pltpu.VMEM),
                pl.BlockSpec(memory_space=pl.ANY),
                pl.BlockSpec(memory_space=pl.ANY),
            ],
            out_specs=pl.BlockSpec(memory_space=pltpu.VMEM),
            scratch_shapes=[
                pltpu.VMEM((groups, 2, 3 * heads * tokens, HEAD_SIZE), jnp.bfloat16),
                pltpu.VMEM((tokens, (2 * heads + 1) * tokens), jnp.float32),
                pltpu.SemaphoreType.DMA((2, groups)),
                pltpu.SemaphoreType.DMA((heads, groups)),
                pltpu.SemaphoreType.DMA((heads, groups)),
                pltpu.SemaphoreType.DMA((groups,)),
                pltpu.SemaphoreType.DMA((groups,)),
                pltpu.SemaphoreType.DMA((groups,)),
                pltpu.SemaphoreType.DMA((groups,)),
            ],
            compiler_params=pltpu.CompilerParams(collective_id=0, has_side_effects=True),
        )(lengths, query, keys, values)

    rows = P(("outer", "inner", "head"), None)
    return jax.shard_map(
        per_device,
        mesh=mesh,
        in_specs=(rows, rows, rows, P()),
        out_specs=rows,
        check_vma=False,
    )
```

time: 249 us -> 85.4 us (0.34)
  Pallas kernels: 0 us -> 81.5 us
  matrix products: 73 us -> 0 us
  blocking collectives: 51 us -> 0 us
  waiting for transfers between devices: 42.7 us -> 0 us
  local copies, waits for them, and re-layouts: 30.7 us -> 3.1 us
  other arithmetic: 25.2 us -> 0 us
  starting transfers between devices: 22.9 us -> 0 us
    pallas_call x0 -> x1, Pallas kernels: none -> 81.5 us  [per_device(): pl.pallas_call(functools.partial(kernel, heads, outers, inners), out_shap...]
    dot_general x48 -> x0, matrix products: 73 us -> none  [the longest x24 59.7 us: one_group(): jnp.einsum('kqc,ckd->qkd', weights.astype(jnp.bfloat16), value_heads, pre...]
    all_to_all x1 -> x0, blocking collectives: 51 us -> none  [per_device(): lax.all_to_all(outcome, 'head', split_axis=0, concat_axis=1, tiled=True)]
    all_to_all x3 -> x0, waiting for transfers between devices: 30.4 us -> none  [the longest x1 17.9 us: per_device(): lax.all_to_all(query, 'head', split_axis=1, concat_axis=0, tiled=True)]
    reduce_sum x25 -> x0, other arithmetic: 13.6 us -> none  [the longest x24 13.5 us: one_group(): new_total = running_total * shrink + jnp.sum(weights, axis=2)]
    all_to_all x3 -> x0, starting transfers between devices: 13.4 us -> none  [the longest x1 6.35 us: per_device(): lax.all_to_all(keys, 'head', split_axis=1, concat_axis=0, tiled=True)]
    ppermute x2 -> x0, waiting for transfers between devices: 12.3 us -> none  [from_behind(): lax.ppermute(value, axis, [(source, source + steps) for source in range(l...]
    ppermute x2 -> x0, starting transfers between devices: 9.49 us -> none  [from_behind(): lax.ppermute(value, axis, [(source, source + steps) for source in range(l...]
  transfers between devices with their start and end apart: 5 -> 0, of which waited for: 5 -> 0; matrix products, arithmetic and copies ran while one was open for 4% -> 0% of each run, Pallas kernels for 0% -> 0%
where the time goes in v1:
time: 85.4 us; the launch traced here: 84.6 us
  Pallas kernels  81.5 us (95%)
  local copies, waits for them, and re-layouts  3.1 us (4%)
    pallas_call x1, Pallas kernels, per_device(): pl.pallas_call(functools.partial(kernel, heads, outers, inners), out_shap...  81.5 us
    unnamed x1, local copies, waits for them, and re-layouts  3.1 us

profile of v1, /device:TPU:0, one launch (start us, length us, event | category | flops | bytes accessed | tf_op | source)
XLA Modules:
  0.0 84.6 jit_solution(3335321896548477565)
XLA Ops:
  0.0 81.5 %shard_map.46 = bf16[128,8192]{1,0:T(8,128)(2,1)} custom-call(s32[8]{0:T(128)} %lengths_ref.1, bf16[128,8192]{1,0:T(8,128)(2,1)} %q_ref.1, bf16[128,1024]{1,0:T(8,128)(2,1)} %k_ref.1, bf16[128,1024]{1,0:T(8,128)(2,1)} %v_ref.1), custom_call_target="tpu_custom_call" | custom-call | tf_op jit(solution)/shard_map/pallas_call | solution.py:195
  81.5 3.1 %copy.6 = bf16[128,8192]{1,0:T(8,128)(2,1)} copy(bf16[128,8192]{1,0:T(8,128)(2,1)} %shard_map.46) | data formatting | bytes 4194304

commit v2 on v1

--- a/solution.py
+++ b/solution.py
@@ -40,49 +40,80 @@
             own_sem.at[which, g],
         )
 
-    def z_copy(g, distance):
-        rows = pl.ds(pl.multiple_of(2 * block + me * tokens, tokens), tokens)
+    def z_copy(g, shard, way):
+        rows = pl.ds(pl.multiple_of(2 * block + shard * tokens, tokens), tokens)
+        slot = jnp.where((way < 0) & (shard == me), heads, shard)
         return pltpu.make_async_remote_copy(
             src_ref=kv.at[g, :, rows, :],
             dst_ref=kv.at[g, :, rows, :],
-            send_sem=z_send.at[distance, g],
-            recv_sem=z_recv.at[distance, g],
-            device_id={"head": lax.rem(me + distance, heads)},
+            send_sem=z_send.at[slot, g],
+            recv_sem=z_recv.at[shard, g],
+            device_id={"head": lax.rem(me + way + heads, heads)},
             device_id_type=MESH,
         )
 
-    def z_arrival(g, distance):
-        source = lax.rem(me - distance + heads, heads)
-        rows = pl.ds(pl.multiple_of(2 * block + source * tokens, tokens), tokens)
+    def has_next(way):
+        return (me + way >= 0) & (me + way < heads)
+
+    def z_onward(g, shard, way):
+        @pl.when(has_next(way))
+        def _():
+            z_copy(g, shard, way).start()
+
+    def z_arrived(g, distance):
+        for way in (1, -1):
+            shard = me - way * distance
+
+            @pl.when((shard >= 0) & (shard < heads))
+            def _():
+                z_copy(g, shard, way).wait_recv()
+                z_onward(g, shard, way)
+                pass_on(g, shard)
+
+    def y_copy(g, shard):
+        rows = pl.ds(pl.multiple_of(2 * block + shard * tokens, tokens), tokens)
+        landing = pl.ds(pl.multiple_of(shard * tokens, tokens), tokens)
         return pltpu.make_async_remote_copy(
             src_ref=kv.at[g, :, rows, :],
-            dst_ref=kv.at[g, :, rows, :],
-            send_sem=z_send.at[distance, g],
-            recv_sem=z_recv.at[distance, g],
-            device_id={"head": lax.rem(me + distance, heads)},
-            device_id_type=MESH,
-        )
-
-    def y_copy(g):
-        return pltpu.make_async_remote_copy(
-            src_ref=kv.at[g, :, pl.ds(2 * block, block), :],
-            dst_ref=kv.at[g, :, pl.ds(0, block), :],
-            send_sem=y_send.at[g],
-            recv_sem=y_recv.at[g],
+            dst_ref=kv.at[g, :, landing, :],
+            send_sem=y_send.at[shard, g],
+            recv_sem=y_recv.at[shard, g],
             device_id=context(2),
             device_id_type=MESH,
         )
 
-    def x_copy(g):
-        start = pl.multiple_of((1 - odd) * 2 * block, block)
+    def x_copy(g, shard):
+        rows = pl.ds(pl.multiple_of((1 - odd) * 2 * block + shard * tokens, tokens), tokens)
+        landing = pl.ds(pl.multiple_of(block + shard * tokens, tokens), tokens)
         return pltpu.make_async_remote_copy(
-            src_ref=kv.at[g, :, pl.ds(start, block), :],
-            dst_ref=kv.at[g, :, pl.ds(block, block), :],
-            send_sem=x_send.at[g],
-            recv_sem=x_recv.at[g],
+            src_ref=kv.at[g, :, rows, :],
+            dst_ref=kv.at[g, :, landing, :],
+            send_sem=x_send.at[shard, g],
+            recv_sem=x_recv.at[shard, g],
             device_id=partner,
             device_id_type=MESH,
         )
+
+    def y_needed(shard):
+        return (odd == 1) | (shard >= me)
+
+    def pass_on(g, shard):
+        @pl.when(y_needed(shard))
+        def _():
+            y_copy(g, shard).start()
+
+        @pl.when(odd == 0)
+        def _():
+            x_copy(g, shard).start()
+
+    def y_arrived(g, shard):
+        @pl.when(y_needed(shard))
+        def _():
+            y_copy(g, shard).wait_recv()
+
+        @pl.when(odd == 1)
+        def _():
+            x_copy(g, shard).start()
 
     for g in range(groups):
         own_copy(g, 0).start()
@@ -100,8 +131,9 @@
     for g in range(groups):
         own_copy(g, 0).wait()
         own_copy(g, 1).wait()
-        for distance in range(1, heads):
-            z_copy(g, distance).start()
+        z_onward(g, me, 1)
+        z_onward(g, me, -1)
+        pass_on(g, me)
 
     first = ctx * block + me * tokens
     query_pos = first + lax.broadcasted_iota(jnp.int32, (tokens, span), 0)
@@ -149,38 +181,48 @@
         lax.fori_loop(0, width // pair, heads_of, 0)
 
     def step(t, carry):
-        @pl.when(t < groups)
-        def _():
-            for distance in range(1, heads):
-                z_arrival(t, distance).wait_recv()
-            y_copy(t).start()
-
-            @pl.when(odd == 0)
-            def _():
-                x_copy(t).start()
-
-        @pl.when((t >= 1) & (t < groups + 1))
-        def _():
-            y_copy(t - 1).wait_recv()
-
-            @pl.when(odd == 1)
-            def _():
-                x_copy(t - 1).start()
-
-        @pl.when(t >= 2)
-        def _():
-            x_copy(t - 2).wait_recv()
-            compute(t - 2)
+        for distance in range(1, heads):
+            @pl.when((t >= distance - 1) & (t < groups + distance - 1))
+            def _():
+                z_arrived(t - distance + 1, distance)
+
+        for distance in range(heads):
+            @pl.when((t >= distance) & (t < groups + distance))
+            def _():
+                for shard in (me - distance, me + distance) if distance else (me,):
+                    @pl.when((shard >= 0) & (shard < heads))
+                    def _():
+                        y_arrived(t - distance, shard)
+
+        @pl.when(t >= heads)
+        def _():
+            for shard in range(heads):
+                x_copy(t - heads, shard).wait_recv()
+            compute(t - heads)
 
         return carry
 
-    lax.fori_loop(0, groups + 2, step, 0)
+    lax.fori_loop(0, groups + heads, step, 0)
 
     def drain(g, carry):
-        for distance in range(1, heads):
-            z_copy(g, distance).wait_send()
-        y_copy(g).wait_send()
-        x_copy(g).wait_send()
+        for way in (1, -1):
+            @pl.when(has_next(way))
+            def _():
+                z_copy(g, me, way).wait_send()
+
+                for distance in range(1, heads):
+                    shard = me - way * distance
+
+                    @pl.when((shard >= 0) & (shard < heads))
+                    def _():
+                        z_copy(g, shard, way).wait_send()
+
+        for shard in range(heads):
+            @pl.when(y_needed(shard))
+            def _():
+                y_copy(g, shard).wait_send()
+
+            x_copy(g, shard).wait_send()
         return carry
 
     lax.fori_loop(0, groups, drain, 0)
@@ -206,12 +248,12 @@
                 pltpu.VMEM((groups, 2, 3 * heads * tokens, HEAD_SIZE), jnp.bfloat16),
                 pltpu.VMEM((tokens, (2 * heads + 1) * tokens), jnp.float32),
                 pltpu.SemaphoreType.DMA((2, groups)),
-                pltpu.SemaphoreType.DMA((heads, groups)),
-                pltpu.SemaphoreType.DMA((heads, groups)),
-                pltpu.SemaphoreType.DMA((groups,)),
-                pltpu.SemaphoreType.DMA((groups,)),
-                pltpu.SemaphoreType.DMA((groups,)),
-                pltpu.SemaphoreType.DMA((groups,)),
+                pltpu.SemaphoreType.DMA((heads + 1, groups)),
+                pltpu.SemaphoreType.DMA((heads, groups)),
+                pltpu.SemaphoreType.DMA((heads, groups)),
+                pltpu.SemaphoreType.DMA((heads, groups)),
+                pltpu.SemaphoreType.DMA((heads, groups)),
+                pltpu.SemaphoreType.DMA((heads, groups)),
             ],
             compiler_params=pltpu.CompilerParams(collective_id=0, has_side_effects=True),
         )(lengths, query, keys, values)

time: 85.4 us -> 81.1 us (0.950)
  Pallas kernels: 81.5 us -> 77.8 us
    pallas_call x1, Pallas kernels: 81.5 us -> 77.8 us  [per_device(): pl.pallas_call(functools.partial(kernel, heads, outers, inners), out_shap...]
where the time goes in v2:
time: 81.1 us; the launch traced here: 80.9 us
  Pallas kernels  77.8 us (96%)
  local copies, waits for them, and re-layouts  3.1 us (4%)
    pallas_call x1, Pallas kernels, per_device(): pl.pallas_call(functools.partial(kernel, heads, outers, inners), out_shap...  77.8 us
    unnamed x1, local copies, waits for them, and re-layouts  3.1 us

profile of v2, /device:TPU:0, one launch (start us, length us, event | category | flops | bytes accessed | tf_op | source)
XLA Modules:
  0.0 80.9 jit_solution(9195801266801615827)
XLA Ops:
  0.0 77.8 %shard_map.46 = bf16[128,8192]{1,0:T(8,128)(2,1)} custom-call(s32[8]{0:T(128)} %lengths_ref.1, bf16[128,8192]{1,0:T(8,128)(2,1)} %q_ref.1, bf16[128,1024]{1,0:T(8,128)(2,1)} %k_ref.1, bf16[128,1024]{1,0:T(8,128)(2,1)} %v_ref.1), custom_call_target="tpu_custom_call" | custom-call | tf_op jit(solution)/shard_map/pallas_call | solution.py:237
  77.8 3.1 %copy.6 = bf16[128,8192]{1,0:T(8,128)(2,1)} copy(bf16[128,8192]{1,0:T(8,128)(2,1)} %shard_map.46) | data formatting | bytes 4194304
